TPU v7x, 32 devices: a whole 2x2x4 slice. The times are simulated.
32 devices in a mesh: heads: 4 (over y, core), blk: 8 (over z, x).
Axes of the slice: x: 2, y: 2, z: 4, core: 2. Of those that a mesh axis runs over, the one named last changes fastest.
Arguments:
- tokens: bfloat16 [4096, 4096], P(('blk', 'heads')), may hold values from -6 to 6
- w_query: bfloat16 [4096, 2048], P('blk', 'heads'), may hold values from -0.75 to 0.75
- key_value_weight: bfloat16 [4096, 2, 512], P('blk', None, 'heads'), may hold values from -0.75 to 0.75
- w_out: bfloat16 [2048, 4096], P(('heads', 'blk')), may hold values from -0.5 to 0.5
- doc_lengths: int32 [16], replicated, may hold values from 1 to 1024, 4096 in all
Outputs:
- attended: bfloat16 [4096, 4096], P(('blk', 'heads'))
Inputs may be any that keep to these rules, and one draw needn't show every extreme that they name: `doc_lengths`: the 16 lengths sum to 4096; the longest document has exactly 1024 tokens.
All inputs are finite; a program needn't handle non-finite values.
Results may differ from a plain program's by a relative error of at most 0.012.
Values may be sent and summed in bfloat16 or wider, within the bound.
A program may use at most 128 MiB of HBM per device.

v0:
```python
import jax
import jax.numpy as jnp
from jax import lax
from jax.sharding import PartitionSpec as P

HEAD_SIZE = 128


norm_epsilon = 1e-05
rope_base = 500000.0
masked_score = -1e30


def shifted(value, axis, steps):
    count = lax.axis_size(axis)
    first, last = (max(0, -steps), min(count, count - steps))
    return lax.ppermute(value, axis, [(source, source + steps) for source in range(first, last)])


def locate_documents(positions, doc_lengths):
    ends = jnp.cumsum(doc_lengths)
    after = positions[:, None] >= ends[None, :]
    ident = jnp.sum(after.astype(jnp.int32), axis=1)
    starts = jnp.sum(jnp.where(after, doc_lengths[None, :], 0), axis=1)
    return (ident, starts)


def apply_rotation(values, relative_offset):
    half = values.shape[-1] // 2
    freqs = jnp.power(rope_base, -2.0 * jnp.arange(half, dtype=jnp.float32) / values.shape[-1])
    angle = relative_offset.astype(jnp.float32)[:, None] * freqs[None, :]
    cosine = jnp.cos(angle)[:, None, :]
    sine = jnp.sin(angle)[:, None, :]
    first = values[..., :half]
    second = values[..., half:]
    return jnp.concatenate(
        [first * cosine - second * sine, second * cosine + first * sine], axis=-1
    )


def on_device(tokens, w_query, key_value_weight, w_out, doc_lengths):
    blk_index = lax.axis_index("blk")
    reach = lax.axis_size("blk") // 4
    values = tokens.astype(jnp.float32)
    normalized_input = (
        values * lax.rsqrt(jnp.mean(values * values, axis=1, keepdims=True) + norm_epsilon)
    ).astype(jnp.bfloat16)
    block_input = lax.all_gather(normalized_input, "heads", axis=0, tiled=True)
    block_rows = block_input.shape[0]
    query_cols = w_query.shape[1]
    kv_cols = key_value_weight.shape[2]
    pieces = (
        lax.all_gather(w_query, "blk", axis=0, tiled=True),
        lax.all_gather(key_value_weight, "blk", axis=0, tiled=True),
    )
    count = pieces[0].shape[0]
    query_part = jnp.dot(block_input, pieces[0], preferred_element_type=jnp.float32)
    keyval_part = jnp.dot(
        block_input, pieces[1].reshape(count, 2 * kv_cols), preferred_element_type=jnp.float32
    )
    positions = blk_index * block_rows + jnp.arange(block_rows, dtype=jnp.int32)
    ident, starts = locate_documents(positions, doc_lengths)
    relative_offset = positions - starts
    query_heads = query_cols // HEAD_SIZE
    kv_heads = kv_cols // HEAD_SIZE
    head_group = query_heads // kv_heads
    query_rows = apply_rotation(
        query_part.reshape(block_rows, query_heads, HEAD_SIZE), relative_offset
    ).astype(jnp.bfloat16)
    query_rows = query_rows.reshape(block_rows, kv_heads, head_group, HEAD_SIZE)
    rotated_keys = apply_rotation(
        keyval_part[:, :kv_cols].reshape(block_rows, kv_heads, HEAD_SIZE), relative_offset
    ).astype(jnp.bfloat16)
    value_rows = (
        keyval_part[:, kv_cols:].reshape(block_rows, kv_heads, HEAD_SIZE).astype(jnp.bfloat16)
    )
    kv_block = jnp.stack([rotated_keys, value_rows], axis=1)
    scale = HEAD_SIZE ** (-0.5)

    def attend_tile(state, kv_now, distance):
        key_pos = (blk_index - distance) * block_rows + jnp.arange(block_rows, dtype=jnp.int32)
        key_doc, unused_k = locate_documents(key_pos, doc_lengths)
        keep = (
            (key_pos[None, :] >= 0)
            & (key_pos[None, :] <= positions[:, None])
            & (key_doc[None, :] == ident[:, None])
        )
        highest, totals, accum = state
        scores = (
            jnp.einsum(
                "qhgd,khd->hgqk", query_rows, kv_now[:, 0], preferred_element_type=jnp.float32
            )
            * scale
        )
        scores = jnp.where(keep, scores, masked_score)
        new_high = jnp.maximum(highest, jnp.max(scores, axis=-1))
        fading = jnp.exp(highest - new_high)
        probs = jnp.where(keep, jnp.exp(scores - new_high[..., None]), 0.0)
        totals = totals * fading + jnp.sum(probs, axis=-1)
        update = jnp.einsum(
            "hgqk,khd->hgqd",
            probs.astype(jnp.bfloat16),
            kv_now[:, 1],
            preferred_element_type=jnp.float32,
        )
        accum = accum * fading[..., None] + update
        return (new_high, totals, accum)

    initial = (
        jnp.full((kv_heads, head_group, block_rows), masked_score, jnp.float32),
        jnp.zeros((kv_heads, head_group, block_rows), jnp.float32),
        jnp.zeros((kv_heads, head_group, block_rows, HEAD_SIZE), jnp.float32),
    )
    state = attend_tile(initial, kv_block, 0)

    def advance(distance, carry):
        kv_now, inner = carry
        kv_now = shifted(kv_now, "blk", 1)
        return (kv_now, attend_tile(inner, kv_now, distance))

    unused_kv, state = lax.fori_loop(1, reach + 1, advance, (kv_block, state))
    highest, totals, accum = state
    mixed = accum / totals[..., None]
    mixed = mixed.transpose(2, 0, 1, 3).reshape(block_rows, query_cols).astype(jnp.bfloat16)
    head_rows = lax.all_gather(w_out, "blk", axis=0, tiled=True)
    return lax.psum_scatter(
        jnp.dot(mixed, head_rows, preferred_element_type=jnp.float32).astype(jnp.bfloat16),
        "heads",
        scatter_dimension=0,
        tiled=True,
    )


def solution(mesh):
    return jax.shard_map(
        on_device,
        mesh=mesh,
        in_specs=(
            P(("blk", "heads"), None),
            P("blk", "heads"),
            P("blk", None, "heads"),
            P(("heads", "blk"), None),
            P(),
        ),
        out_specs=P(("blk", "heads"), None),
        check_vma=False,
    )
```

profile of v0, /device:TPU:27, one launch (start us, length us, event | category | flops | bytes accessed | tf_op | source)
XLA Modules:
  0.0 309.9 jit_solution(1493680241664175790)
XLA Ops:
  6.5 0.7 all-gather.7.cloned.1.call-update
  7.3 0.0 all-gather.5.cloned.1.call-start
  7.3 1.5 fusion.24
  8.8 2.5 fusion.25
  11.3 0.0 all-gather.9.cloned.1.call-start
  11.4 0.7 all-gather.9.cloned.1.call-update
  12.1 0.5 all-gather.11.cloned.1.call-update
  12.6 0.0 reduce-scatter.2.cloned.1.call-start
  12.7 0.2 broadcast_in_dim.114
  12.9 0.1 fusion.56
  13.0 1.0 multiply_cosine_fusion
  14.0 0.3 compare_and_fusion.1
  14.4 42.2 %all-gather.7.cloned.1.call-done = bf16[4096,2,128]{2,1,0:T(2,128)(2,1)} async-done(((bf16[512,2,128]{2,1,0:T(2,128)(2,1)}), bf16[4096,2,128]{2,1,0:T(2,128)(2,1)}) %all-gather.7.cloned.1.call-update) | async-done | bytes 2097168 | tf_op jit(solution)/shard_map/all_gather | solution.py:54
  56.6 37.9 %all-gather.5.cloned.1.call-done = bf16[512,4096]{1,0:T(8,128)(2,1)} async-done(((bf16[128,4096]{1,0:T(8,128)(2,1)}), bf16[512,4096]{1,0:T(8,128)(2,1)}) %all-gather.5.cloned.1.call-update) | async-done | bytes 4194320 | tf_op jit(solution)/shard_map/all_gather | solution.py:48
  94.5 4.2 %fusion.27 = f32[512,256]{0,1:T(8,128)S(1)} fusion(bf16[512,4096]{1,0:T(8,128)(2,1)} %all-gather.5.cloned.1.call-done, bf16[512,8,2,128]{3,2,1,0:T(2,128)(2,1)} %bitcast.161), kind=kOutput, calls=%fused_computation.38 | convolution fusion | flops 1073741824 | bytes 6815744 | tf_op jit(solution)/shard_map/dot_general | solution.py:58
  98.7 0.6 fusion.48
  99.3 0.2 copy-done
  99.5 0.8 copy.35
  100.3 66.3 %all-gather.9.cloned.1.call-done = bf16[4096,512]{1,0:T(8,128)(2,1)} async-done(((bf16[512,512]{1,0:T(8,128)(2,1)}), bf16[4096,512]{1,0:T(8,128)(2,1)}) %all-gather.9.cloned.1.call-update) | async-done | bytes 4194320 | tf_op jit(solution)/shard_map/all_gather | solution.py:53
  166.7 5.8 %fusion.64 = f32[512,512]{0,1:T(8,128)S(1)} fusion(bf16[512,4096]{1,0:T(8,128)(2,1)} %all-gather.5.cloned.1.call-done, bf16[4096,512]{1,0:T(8,128)(2,1)} %all-gather.9.cloned.1.call-done), kind=kOutput, calls=%fused_computation.92 | convolution fusion | flops 2147483648 | bytes 9437184 | tf_op jit(solution)/shard_map/dot_general | solution.py:57
  172.5 0.1 fusion.63
  172.6 0.3 copy.43
  173.0 0.3 copy.44
  173.3 0.3 subtract_convert_fusion
  173.6 0.3 pad_maximum_fusion
  173.9 1.2 fusion.21
  175.1 1.0 fusion.23
  176.2 1.6 fusion.36
  177.8 42.3 %while.22 = (s32[]{:T(128)}, bf16[512,2,1,128]{3,0,2,1:T(8,128)(2,1)S(1)}, f32[1,4,512]{2,1,0:T(4,128)S(1)}, f32[1,4,512]{2,1,0:T(4,128)S(1)}, f32[1,4,512,128]{...) while((s32[]{:T(128)}, ...), condition=%wide.region_10.11_spmd.clone, body=%wide.region_6.10_spmd.clone.sunk | while | flops 552107520 | bytes 18236672 | solution.py:121
  178.0 1.3 collective-permute-start
  179.3 0.1 convert_reduce_fusion.2
  179.4 0.3 compare_and_fusion.3
  179.8 11.0 %collective-permute-done = bf16[512,2,1,128]{3,0,2,1:T(8,128)(2,1)S(1)} collective-permute-done((bf16[512,2,1,128]{3,0,2,1:T(8,128)(2,1)S(1)}, bf16[512,2,1,128]{3,0,2,1:T(8,128)(2,1)S(1)}, u32[]{:S(2)}, u32[]{:S(2)}) %collective-permute-start) | collective-permute-done | bytes 262176 | tf_op jit(solution)/shard_map/while/body/eval_jaxpr/ppermute | solution.py:17
  190.7 0.9 fusion.76
  191.6 1.0 fusion.78
  192.7 1.9 fusion.79
  194.7 1.3 collective-permute-start
  196.0 0.1 convert_reduce_fusion.2
  196.1 0.3 compare_and_fusion.3
  196.4 19.7 %collective-permute-done = bf16[512,2,1,128]{3,0,2,1:T(8,128)(2,1)S(1)} collective-permute-done((bf16[512,2,1,128]{3,0,2,1:T(8,128)(2,1)S(1)}, bf16[512,2,1,128]{3,0,2,1:T(8,128)(2,1)S(1)}, u32[]{:S(2)}, u32[]{:S(2)}) %collective-permute-start) | collective-permute-done | bytes 262176 | tf_op jit(solution)/shard_map/while/body/eval_jaxpr/ppermute | solution.py:17
  216.2 0.9 fusion.76
  217.1 1.0 fusion.78
  218.2 1.9 fusion.79
  220.1 0.3 copy.36
  220.4 0.1 divide_convert_fusion
  220.6 30.2 %all-gather.11.cloned.1.call-done = bf16[512,4096]{1,0:T(8,128)(2,1)} async-done(((bf16[64,4096]{1,0:T(8,128)(2,1)}), bf16[512,4096]{1,0:T(8,128)(2,1)}) %all-gather.11.cloned.1.call-update) | async-done | bytes 4194320 | tf_op jit(solution)/shard_map/all_gather | solution.py:125
  250.8 6.5 %convolution_convert_fusion = bf16[512,4096]{1,0:T(8,128)(2,1)} fusion(bf16[512,512]{0,1:T(8,128)(2,1)S(1)} %bitcast.151, bf16[512,4096]{1,0:T(8,128)(2,1)} %all-gather.11.cloned.1.call-done), kind=kOutput, calls=%fused_computation.27 | convolution fusion | flops 2149580800 | bytes 8912896 | tf_op jit(solution)/shard_map/dot_general | solution.py:127
  257.3 46.0 %reduce-scatter.2.cloned.1.call-done = bf16[128,4096]{1,0:T(8,128)(2,1)} async-done(((bf16[512,4096]{1,0:T(8,128)(2,1)}), bf16[128,4096]{1,0:T(8,128)(2,1)}) %reduce-scatter.2.cloned.1.call-update) | async-done | bytes 1048592 | tf_op jit(solution)/shard_map/reduce_scatter | solution.py:126
  (33 shorter events, 0.3 us)
Async XLA Ops:
  6.5 6.2 %copy-start.3 = (s32[16]{0:T(128)S(1)}, s32[16]{0:T(128)}, u32[]{:S(2)}) copy-start(s32[16]{0:T(128)} %param.11) | copy-start | bytes 196
  6.5 50.0 %all-gather.7.cloned.1.call-start = ((), (), s32[]{:S(2)}) async-start(), calls=%async_computation.2 | async-start | bytes 2359296 | tf_op jit(solution)/shard_map/all_gather | solution.py:54
  7.3 87.3 %all-gather.5.cloned.1.call-start = ((), (), s32[]{:S(2)}) async-start(), calls=%async_computation.1 | async-start | bytes 5242880 | tf_op jit(solution)/shard_map/all_gather | solution.py:48
  11.3 155.3 %all-gather.9.cloned.1.call-start = ((), (), s32[]{:S(2)}) async-start(), calls=%async_computation.3 | async-start | bytes 4718592 | tf_op jit(solution)/shard_map/all_gather | solution.py:53
  12.1 238.7 %all-gather.11.cloned.1.call-start = ((), (), s32[]{:S(2)}) async-start(), calls=%async_computation.4 | async-start | bytes 4718592 | tf_op jit(solution)/shard_map/all_gather | solution.py:125
  12.6 290.7 %reduce-scatter.2.cloned.1.call-start = ((), (), s32[]{:S(2)}) async-start(), calls=%async_computation.5 | async-start | bytes 5242880 | tf_op jit(solution)/shard_map/reduce_scatter | solution.py:126
  98.7 0.8 copy-start
  173.9 2.3 copy-start.1
  176.2 1.6 copy-start.2
  178.0 12.7 %collective-permute-start = (bf16[512,2,1,128]{3,0,2,1:T(8,128)(2,1)S(1)}, bf16[512,2,1,128]{3,0,2,1:T(8,128)(2,1)S(1)}, u32[]{:S(2)}, u32[]{:S(2)}) collective-permute-start(bf16[512,2,1,128]{3,0,2,1:T(8,128)(2,1)S(1)} %get-tuple-element.431), channel_id=1, source_target_pairs={{0,1},{1,2},{2,3},{3,4},{4,5},{5,6},{6,7},{8,9},{9,10},{10,11},{11... | collective-permute-start | bytes 786440 | tf_op jit(solution)/shard_map/while/body/eval_jaxpr/ppermute | solution.py:17
  194.7 21.5 %collective-permute-start = (bf16[512,2,1,128]{3,0,2,1:T(8,128)(2,1)S(1)}, bf16[512,2,1,128]{3,0,2,1:T(8,128)(2,1)S(1)}, u32[]{:S(2)}, u32[]{:S(2)}) collective-permute-start(bf16[512,2,1,128]{3,0,2,1:T(8,128)(2,1)S(1)} %get-tuple-element.431), channel_id=1, source_target_pairs={{0,1},{1,2},{2,3},{3,4},{4,5},{5,6},{6,7},{8,9},{9,10},{10,11},{11... | collective-permute-start | bytes 786440 | tf_op jit(solution)/shard_map/while/body/eval_jaxpr/ppermute | solution.py:17
Sparse Core Ops, SparseCore 0:
  9.5 47.0 all-gather.6
  58.1 36.3 all-gather.4
  96.6 69.9 all-gather.8
  168.6 82.0 all-gather.10
  257.4 45.8 reduce-scatter.1
where the time goes:
time: 312 us; the launch traced here: 310 us
  waiting for transfers between devices  255 us (82%)
  matrix products  24.9 us (8%)
  between operations  13.4 us (4%)
  other arithmetic  11 us (4%)
    all_gather x1, waiting for transfers between devices, on_device(): lax.all_gather(w_query, 'blk', axis=0, tiled=True)  66.3 us
    reduce_scatter x1, waiting for transfers between devices, on_device(): lax.psum_scatter(jnp.dot(mixed, head_rows, preferred_element_type=jnp.flo...  46 us
    all_gather x1, waiting for transfers between devices, on_device(): lax.all_gather(key_value_weight, 'blk', axis=0, tiled=True)  42.2 us
    all_gather x1, waiting for transfers between devices, on_device(): block_input = lax.all_gather(normalized_input, 'heads', axis=0, tiled=True)  37.9 us
    ppermute x2, waiting for transfers between devices, shifted(): lax.ppermute(value, axis, [(source, source + steps) for source in range(f...  30.7 us
    all_gather x1, waiting for transfers between devices, on_device(): head_rows = lax.all_gather(w_out, 'blk', axis=0, tiled=True)  30.2 us
    dot_general x1, matrix products, on_device(): jnp.dot(mixed, head_rows, preferred_element_type=jnp.float32)  6.52 us
  transfers between devices with their start and end apart: 7, of which 7 were waited for; matrix products, arithmetic and copies ran while one was open for 10% of the time, Pallas kernels for 0%

commit v1 on v0

v1 whole, which is shorter than its diff:
```python
import functools

import jax
import jax.numpy as jnp
from jax import lax
from jax.experimental import pallas as pl
from jax.experimental.pallas import tpu as pltpu
from jax.sharding import PartitionSpec as P

HEAD_SIZE = 128
CHUNKS = 2
LINE = 2

norm_epsilon = 1e-05
rope_base = 500000.0
masked_score = -1e30
MESH = pl.DeviceIdType.MESH
UP, DOWN, ACROSS = 0, 1, 2


def layer_kernel(
    n, heads, chunks,
    tok_ref, w_in_ref, w_out_ref, len_ref, freq_ref, out_ref,
    w_in, w_proj, acts, qkv, query, kv, high, total, accum, mixed, rope,
    near_send, near_recv, part, far_send, far_recv,
    local_sem, in_send, in_recv, proj_send, proj_recv, bal_send,
    act_send, act_recv, kv_send, kv_recv, near_ss, near_rs, far_ss, far_rs,
):
    f32, bf16 = jnp.float32, jnp.bfloat16
    b = lax.axis_index("blk")
    h = lax.axis_index("heads")
    steps = n // LINE
    z, x = b // LINE, b % LINE
    outer = heads // 2
    y, core = h // 2, h % 2
    mate = y * 2 + 1 - core
    reach = n // 4
    tokens_own, width = tok_ref.shape
    rows_in, in_cols = w_in_ref.shape
    rows_out = w_out_ref.shape[0]
    chunk_cols = w_out_ref.shape[1] // chunks
    block = tokens_own * heads
    q_cols = query.shape[1]
    q_heads = q_cols // HEAD_SIZE

    def at_blk(i):
        return {"blk": i}

    def at_head(i):
        return {"heads": i}

    def remote(src, dst, ss, rs, dev):
        return pltpu.make_async_remote_copy(
            src_ref=src, dst_ref=dst, send_sem=ss, recv_sem=rs, device_id=dev, device_id_type=MESH
        )

    barrier = pltpu.get_barrier_semaphore()
    span = max(reach, LINE)
    peers = 0
    for d in sorted({e % n for k in range(1, span + 1) for e in (k, -k)}):
        pl.semaphore_signal(barrier, inc=1, device_id=at_blk(lax.rem(b + d, n)), device_id_type=MESH)
        peers += 1
    for d in range(1, heads):
        pl.semaphore_signal(barrier, inc=1, device_id=at_head(lax.rem(h + d, heads)), device_id_type=MESH)
        peers += 1
    pl.semaphore_wait(barrier, peers)

    def in_slot(i):
        return w_in.at[pl.ds(pl.multiple_of(i * rows_in, rows_in), rows_in)]

    def proj_slot(c, i):
        return w_proj.at[c, i]

    def proj_own(c):
        return w_out_ref.at[:, pl.ds(c * chunk_cols, chunk_cols)]

    def stream(c):
        if c < 0:
            return in_slot, w_in_ref, lambda d, r: in_send.at[d, r], lambda i: in_recv.at[i]
        return (
            functools.partial(proj_slot, c), proj_own(c),
            lambda d, r: proj_send.at[c, d, r], lambda i: proj_recv.at[c, i],
        )

    def target(direction):
        if direction == UP:
            return at_blk(lax.rem(b + LINE, n))
        if direction == DOWN:
            return at_blk(lax.rem(b + n - LINE, n))
        return at_blk(z * LINE + 1 - x)

    def send_copy(c, direction, row, own):
        slot, source, ss, rs = stream(c)
        origin = row * LINE + x
        dst = slot(origin)
        return remote(source if own else dst, dst, ss(direction, row), rs(origin), target(direction))

    def await_slot(c, origin):
        slot, source, ss, rs = stream(c)
        ref = slot(origin)
        remote(ref, ref, ss(0, 0), rs(origin), target(ACROSS)).wait_recv()

    def crosses(c, row):
        if c < 0:
            return row >= 0
        return jnp.logical_not(((z == 0) & (row == 1)) | ((z == steps - 1) & (row == steps - 2)))

    def line_own(c):
        @pl.when(z < steps - 1)
        def _():
            send_copy(c, UP, z, True).start()

        @pl.when(z > 0)
        def _():
            send_copy(c, DOWN, z, True).start()

    def line_step(c, s):
        @pl.when(z - s >= 0)
        def _():
            await_slot(c, (z - s) * LINE + x)

            @pl.when(z < steps - 1)
            def _():
                send_copy(c, UP, z - s, False).start()

        @pl.when(z + s <= steps - 1)
        def _():
            await_slot(c, (z + s) * LINE + x)

            @pl.when(z > 0)
            def _():
                send_copy(c, DOWN, z + s, False).start()

    def cross_own(c):
        send_copy(c, ACROSS, z, True).start()

    def cross_step(c, s):
        @pl.when((z - s >= 0) & crosses(c, z - s))
        def _():
            send_copy(c, ACROSS, z - s, False).start()

        @pl.when((z + s <= steps - 1) & crosses(c, z + s))
        def _():
            send_copy(c, ACROSS, z + s, False).start()

    def side_copy(c, end):
        ref = proj_slot(c, z * LINE + 1 - x)
        return remote(ref, ref, bal_send.at[c, end], proj_recv.at[c, z * LINE + 1 - x],
                      target(DOWN if end == 0 else UP))

    def balance(c):
        @pl.when((z == 1) | (z == steps - 2))
        def _():
            await_slot(c, z * LINE + 1 - x)

        @pl.when(z == 1)
        def _():
            side_copy(c, 0).start()

        @pl.when(z == steps - 2)
        def _():
            side_copy(c, 1).start()

    def await_crossed(c):
        def one(row, _):
            already = ((z == 1) | (z == steps - 2)) & (row == z) & (c >= 0)

            @pl.when(jnp.logical_not(already))
            def _():
                await_slot(c, row * LINE + 1 - x)
            return 0

        lax.fori_loop(0, steps, one, 0)

    line_own(-1)
    cross_own(-1)
    keep_in = pltpu.make_async_copy(w_in_ref, in_slot(b), local_sem.at[chunks])
    keep_in.start()
    keep_out = [
        pltpu.make_async_copy(proj_own(c), proj_slot(c, b), local_sem.at[c]) for c in range(chunks)
    ]
    for copy in keep_out:
        copy.start()

    values = tok_ref[...].astype(f32)
    acts[h] = (
        values * lax.rsqrt(jnp.mean(values * values, axis=1, keepdims=True) + norm_epsilon)
    ).astype(bf16)

    act_copies = []
    for o in range(1, outer):
        act_copies.append(remote(acts.at[h], acts.at[h], act_send.at[o], act_recv.at[h],
                                 at_head(lax.rem(y + o, outer) * 2 + core)))
    act_copies.append(remote(acts.at[h], acts.at[h], act_send.at[0], act_recv.at[h], at_head(mate)))
    for copy in act_copies:
        copy.start()

    pos = b * block + lax.broadcasted_iota(jnp.int32, (block, 1), 0)
    start = jnp.zeros((block, 1), jnp.int32)
    end = jnp.int32(0)
    for i in range(len_ref.shape[0]):
        size = len_ref[i]
        end = end + size
        start = start + jnp.where(pos >= end, size, 0)
    angle = (pos - start).astype(f32) * freq_ref[...]
    lane = lax.broadcasted_iota(jnp.int32, (block, HEAD_SIZE), 1)
    rope[0] = jnp.cos(angle)
    rope[1] = jnp.where(lane < HEAD_SIZE // 2, -jnp.sin(angle), jnp.sin(angle))

    def in_step(s, _):
        line_step(-1, s)
        cross_step(-1, s)
        return 0

    in_step(1, 0)
    for o in range(1, outer):
        other = lax.rem(y + o, outer) * 2 + core
        remote(acts.at[other], acts.at[other], act_send.at[0], act_recv.at[other], at_head(mate)).wait_recv()
        copy = remote(acts.at[other], acts.at[other], act_send.at[outer + o], act_recv.at[other], at_head(mate))
        copy.start()
        act_copies.append(copy)
    lax.fori_loop(2, steps, in_step, 0)

    for c in range(chunks):
        line_own(c)
    cross_own(0)
    line_events = [(c, s) for s in range(1, steps) for c in range(chunks)]

    def run_events(count):
        for _ in range(min(count, len(line_events))):
            c, s = line_events.pop(0)
            line_step(c, s)
            if c == 0:
                cross_step(0, s)

    run_events(2 * chunks - 1)

    keep_in.wait()
    await_crossed(-1)
    for o in range(outer):
        other = lax.rem(y + o, outer) * 2 + 1 - core
        remote(acts.at[other], acts.at[other], act_send.at[0], act_recv.at[other], at_head(mate)).wait_recv()

    depth = min(512, width)

    def project(k, _):
        cols = pl.ds(pl.multiple_of(k * depth, depth), depth)
        left = acts[:, :, cols].reshape(block, depth)
        term = jnp.dot(left, w_in[cols, :], preferred_element_type=f32)
        qkv[...] = term + qkv[...]
        return 0

    qkv[...] = jnp.zeros_like(qkv)
    lax.fori_loop(0, width // depth, project, 0)

    cosine, sine = rope[0], rope[1]

    def rotated(first):
        v = qkv[:, first:first + HEAD_SIZE]
        return (v * cosine + pltpu.roll(v, HEAD_SIZE // 2, 1) * sine).astype(bf16)

    kv[0, :, :HEAD_SIZE] = rotated(q_cols)
    kv[0, :, HEAD_SIZE:] = qkv[:, q_cols + HEAD_SIZE:].astype(bf16)
    for j in range(q_heads):
        query[:, j * HEAD_SIZE:(j + 1) * HEAD_SIZE] = rotated(j * HEAD_SIZE)

    def kv_copy(d):
        return remote(kv.at[0], kv.at[d], kv_send.at[d], kv_recv.at[d], at_blk(lax.rem(b + d, n)))

    def kv_start(d, _):
        @pl.when(b + d < n)
        def _():
            kv_copy(d).start()
        return 0

    lax.fori_loop(1, reach + 1, kv_start, 0)
    run_events(chunks)

    scale = HEAD_SIZE ** (-0.5)
    high[...] = jnp.full_like(high, masked_score)
    total[...] = jnp.zeros_like(total)
    accum[...] = jnp.zeros_like(accum)
    own_pos = lax.broadcasted_iota(jnp.int32, (block, 1), 0)
    own_start = start - b * block
    key_lane = lax.broadcasted_iota(jnp.int32, (1, block), 1)

    def attend(d):
        key_pos = key_lane - d * block
        keep = (key_pos >= own_start) & (key_pos <= own_pos)

        def one(j, _):
            cols = pl.ds(pl.multiple_of(j * HEAD_SIZE, HEAD_SIZE), HEAD_SIZE)
            scores = lax.dot_general(
                query[:, cols], kv[d, :, :HEAD_SIZE], (((1,), (1,)), ((), ())),
                preferred_element_type=f32,
            ) * scale
            scores = jnp.where(keep, scores, masked_score)
            old = high[j]
            new = jnp.maximum(old, jnp.max(scores, axis=1, keepdims=True))
            fading = jnp.exp(old - new)
            probs = jnp.where(keep, jnp.exp(scores - new), 0.0)
            total[j] = total[j] * fading + jnp.sum(probs, axis=1, keepdims=True)
            update = jnp.dot(probs.astype(bf16), kv[d, :, HEAD_SIZE:], preferred_element_type=f32)
            accum[:, cols] = accum[:, cols] * fading + update
            high[j] = new
            return 0

        lax.fori_loop(0, q_heads, one, 0)

    attend(0)
    run_events(len(line_events))
    balance(0)
    for c in range(1, chunks):
        cross_own(c)
        for s in range(1, steps):
            cross_step(c, s)

    def earlier(d, _):
        @pl.when(b >= d)
        def _():
            remote(kv.at[d], kv.at[d], kv_send.at[d], kv_recv.at[d], at_blk(lax.rem(b + 1, n))).wait_recv()
            attend(d)
        return 0

    lax.fori_loop(1, reach + 1, earlier, 0)

    for g in range(heads):
        rows = slice(g * tokens_own, (g + 1) * tokens_own)
        for j in range(q_heads):
            cols = slice(j * HEAD_SIZE, (j + 1) * HEAD_SIZE)
            mixed[g % 2, g // 2, :, cols] = (accum[rows, cols] / total[j, rows]).astype(bf16)

    tile = min(512, chunk_cols)

    def weight_tile(c, cols):
        right = w_proj[c, :, :, cols]
        if rows_out % 16:
            return right.astype(f32).reshape(n * rows_out, tile).astype(bf16)
        return right.reshape(n * rows_out, tile)

    def near_copy(c):
        return remote(near_send.at[c], near_recv.at[c], near_ss.at[c], near_rs.at[c], at_head(mate))

    def far_copy(c, o):
        other = lax.rem(y + o, outer)
        return remote(far_send.at[c, o], far_recv.at[c, o], far_ss.at[c, o], far_rs.at[c, o],
                      at_head(other * 2 + core))

    def project_out(c):
        keep_out[c].wait()
        await_crossed(c)

        def theirs(k, _):
            cols = pl.ds(pl.multiple_of(k * tile, tile), tile)
            left = mixed[1 - core].reshape(outer * tokens_own, q_cols)
            term = jnp.dot(left, weight_tile(c, cols), preferred_element_type=f32)
            near_send[c, :, :, cols] = term.astype(bf16).reshape(outer, tokens_own, tile)
            return 0

        def ours(k, _):
            cols = pl.ds(pl.multiple_of(k * tile, tile), tile)
            left = mixed[core].reshape(outer * tokens_own, q_cols)
            term = jnp.dot(left, weight_tile(c, cols), preferred_element_type=f32)
            part[c, :, :, cols] = term.reshape(outer, tokens_own, tile)
            return 0

        lax.fori_loop(0, chunk_cols // tile, theirs, 0)
        near_copy(c).start()
        lax.fori_loop(0, chunk_cols // tile, ours, 0)
        near_copy(c).wait_recv()
        for o in range(1, outer):
            other = lax.rem(y + o, outer)
            far_send[c, o] = (part[c, other] + near_recv[c, other].astype(f32)).astype(bf16)
            far_copy(c, o).start()

    def finish(c):
        result = part[c, y] + near_recv[c, y].astype(f32)
        for o in range(1, outer):
            far_copy(c, o).wait_recv()
            result = result + far_recv[c, o].astype(f32)
        out_ref[:, c * chunk_cols:(c + 1) * chunk_cols] = result.astype(bf16)

    for c in range(chunks):
        project_out(c)
        if c + 1 < chunks:
            balance(c + 1)
        if c > 0:
            finish(c - 1)
    finish(chunks - 1)

    def drain(c):
        def one(row, _):
            @pl.when((row <= z) & (z < steps - 1))
            def _():
                send_copy(c, UP, row, False).wait_send()

            @pl.when((row >= z) & (z > 0))
            def _():
                send_copy(c, DOWN, row, False).wait_send()

            @pl.when(crosses(c, row))
            def _():
                send_copy(c, ACROSS, row, False).wait_send()
            return 0

        lax.fori_loop(0, steps, one, 0)

    for c in range(-1, chunks):
        drain(c)
    for c in range(chunks):
        @pl.when(z == 1)
        def _():
            side_copy(c, 0).wait_send()

        @pl.when(z == steps - 2)
        def _():
            side_copy(c, 1).wait_send()

        near_copy(c).wait_send()
        for o in range(1, outer):
            far_copy(c, o).wait_send()
    for copy in act_copies:
        copy.wait_send()

    def kv_drain(d, _):
        @pl.when(b + d < n)
        def _():
            kv_copy(d).wait_send()
        return 0

    lax.fori_loop(1, reach + 1, kv_drain, 0)


def on_device(tokens, w_query, key_value_weight, w_out, doc_lengths):
    n = lax.axis_size("blk")
    heads = lax.axis_size("heads")
    chunks = CHUNKS
    outer = heads // 2
    steps = n // LINE
    own, width = tokens.shape
    block = own * heads
    rows_in, q_cols = w_query.shape
    kv_cols = 2 * key_value_weight.shape[2]
    rows_out = w_out.shape[0]
    chunk_cols = width // chunks
    q_heads = q_cols // HEAD_SIZE
    reach = n // 4
    w_in = jnp.concatenate([w_query, key_value_weight.reshape(rows_in, kv_cols)], axis=1)
    half = HEAD_SIZE // 2
    freqs = jnp.power(rope_base, -2.0 * jnp.arange(half, dtype=jnp.float32) / HEAD_SIZE)
    freqs = jnp.concatenate([freqs, freqs])[None, :]
    bf16, f32 = jnp.bfloat16, jnp.float32
    dma = pltpu.SemaphoreType.DMA
    return pl.pallas_call(
        functools.partial(layer_kernel, n, heads, chunks),
        out_shape=jax.ShapeDtypeStruct((own, width), bf16),
        in_specs=[
            pl.BlockSpec(memory_space=pltpu.VMEM),
            pl.BlockSpec(memory_space=pl.ANY),
            pl.BlockSpec(memory_space=pl.ANY),
            pl.BlockSpec(memory_space=pltpu.SMEM),
            pl.BlockSpec(memory_space=pltpu.VMEM),
        ],
        out_specs=pl.BlockSpec(memory_space=pltpu.VMEM),
        scratch_shapes=[
            pltpu.VMEM((n * rows_in, q_cols + kv_cols), bf16),
            pltpu.VMEM((chunks, n, rows_out, chunk_cols), bf16),
            pltpu.VMEM((heads, own, width), bf16),
            pltpu.VMEM((block, q_cols + kv_cols), f32),
            pltpu.VMEM((block, q_cols), bf16),
            pltpu.VMEM((reach + 1, block, kv_cols), bf16),
            pltpu.VMEM((q_heads, block, 1), f32),
            pltpu.VMEM((q_heads, block, 1), f32),
            pltpu.VMEM((block, q_cols), f32),
            pltpu.VMEM((2, outer, own, q_cols), bf16),
            pltpu.VMEM((2, block, HEAD_SIZE), f32),
            pltpu.VMEM((chunks, outer, own, chunk_cols), bf16),
            pltpu.VMEM((chunks, outer, own, chunk_cols), bf16),
            pltpu.VMEM((chunks, outer, own, chunk_cols), f32),
            pltpu.VMEM((chunks, outer, own, chunk_cols), bf16),
            pltpu.VMEM((chunks, outer, own, chunk_cols), bf16),
            dma((chunks + 1,)),
            dma((3, steps)),
            dma((n,)),
            dma((chunks, 3, steps)),
            dma((chunks, n)),
            dma((chunks, 2)),
            dma((2 * outer,)),
            dma((heads,)),
            dma((reach + 1,)),
            dma((reach + 1,)),
            dma((chunks,)),
            dma((chunks,)),
            dma((chunks, outer)),
            dma((chunks, outer)),
        ],
        compiler_params=pltpu.CompilerParams(
            collective_id=0, has_side_effects=True, vmem_limit_bytes=60 * 1024 * 1024
        ),
    )(tokens, w_in, w_out, doc_lengths, freqs)


def solution(mesh):
    return jax.shard_map(
        on_device,
        mesh=mesh,
        in_specs=(
            P(("blk", "heads"), None),
            P("blk", "heads"),
            P("blk", None, "heads"),
            P(("heads", "blk"), None),
            P(),
        ),
        out_specs=P(("blk", "heads"), None),
        check_vma=False,
    )
```

time: 312 us -> 152 us (0.49)
  waiting for transfers between devices: 255 us -> 0 us
  Pallas kernels: 0 us -> 145 us
  matrix products: 24.9 us -> 0 us
  between operations: 13.4 us -> 0.01 us
  other arithmetic: 11 us -> 2.65 us
    all_gather x4 -> x0, waiting for transfers between devices: 177 us -> none  [the longest x1 66.3 us: on_device(): lax.all_gather(w_query, 'blk', axis=0, tiled=True)]
    pallas_call x0 -> x1, Pallas kernels: none -> 145 us  [on_device(): pl.pallas_call(functools.partial(layer_kernel, n, heads, chunks), out_sha...]
    reduce_scatter x1 -> x0, waiting for transfers between devices: 46 us -> none  [on_device(): lax.psum_scatter(jnp.dot(mixed, head_rows, preferred_element_type=jnp.flo...]
    ppermute x2 -> x0, waiting for transfers between devices: 30.7 us -> none  [shifted(): lax.ppermute(value, axis, [(source, source + steps) for source in range(f...]
    dot_general x9 -> x0, matrix products: 24.9 us -> none  [the longest x1 6.52 us: on_device(): jnp.dot(mixed, head_rows, preferred_element_type=jnp.float32)]
    reduce_sum x7 -> x0, other arithmetic: 4.92 us -> none  [the longest x3 3.13 us: attend_tile(): totals = totals * fading + jnp.sum(probs, axis=-1)]
  transfers between devices with their start and end apart: 7 -> 0, of which waited for: 7 -> 0; matrix products, arithmetic and copies ran while one was open for 10% -> 0% of each run, Pallas kernels for 0% -> 0%
where the time goes in v1:
time: 152 us; the launch traced here: 151 us
  Pallas kernels  145 us (95%)
  local copies, waits for them, and re-layouts  3.27 us (2%)
  other arithmetic  2.65 us (2%)
    pallas_call x1, Pallas kernels, on_device(): pl.pallas_call(functools.partial(layer_kernel, n, heads, chunks), out_sha...  145 us
    unnamed x2, local copies, waits for them, and re-layouts  3.27 us

profile of v1, /device:TPU:27, one launch (start us, length us, event | category | flops | bytes accessed | tf_op | source)
XLA Modules:
  0.0 150.8 jit_solution(13189514120814835164)
XLA Ops:
  0.0 0.7 maximum_bitcast_fusion.freq_ref
  0.7 1.0 copy.8
  1.7 2.0 %pad_maximum_fusion.w_in_ref = bf16[512,768]{1,0:T(8,128)(2,1)} fusion(bf16[512,256]{1,0:T(8,128)(2,1)S(1)} %bitcast.6, bf16[512,512]{1,0:T(8,128)(2,1)} %param.6), kind=kLoop, calls=%fused_computation | loop fusion | flops 1572864 | bytes 1572864 | tf_op jit(solution)/shard_map/concatenate | solution.py:448
  3.6 144.9 %shard_map.55 = bf16[128,4096]{1,0:T(8,128)(2,1)} custom-call(bf16[128,4096]{1,0:T(8,128)(2,1)} %tok_ref.1, bf16[512,768]{1,0:T(8,128)(2,1)} %pad_maximum_fusion.w_in_ref, bf16[64,4096]{1,0:T(8,128)(2,1)} %w_out_ref.1, s32[16]{0:T(128)} %len_ref.1, f32[1,128]{1,0:T(1,128)} %maximum_bitcast_fusion.freq_ref), custom_call_target="tpu_custom_call" | custom-call | tf_op jit(solution)/shard_map/pallas_call | solution.py:454
  148.6 2.3 %copy.10 = bf16[128,4096]{1,0:T(8,128)(2,1)} copy(bf16[128,4096]{1,0:T(8,128)(2,1)} %shard_map.55) | data formatting | bytes 2097152
  (1 shorter events, 0.0 us)

commit v2 on v1

--- a/solution.py
+++ b/solution.py
@@ -2,13 +2,14 @@
 
 import jax
 import jax.numpy as jnp
+import numpy as np
 from jax import lax
 from jax.experimental import pallas as pl
 from jax.experimental.pallas import tpu as pltpu
 from jax.sharding import PartitionSpec as P
 
 HEAD_SIZE = 128
-CHUNKS = 2
+CHUNKS = 4
 LINE = 2
 
 norm_epsilon = 1e-05
@@ -16,12 +17,13 @@
 masked_score = -1e30
 MESH = pl.DeviceIdType.MESH
 UP, DOWN, ACROSS = 0, 1, 2
+QUERY, KEYVAL = -1, -2
 
 
 def layer_kernel(
     n, heads, chunks,
-    tok_ref, w_in_ref, w_out_ref, len_ref, freq_ref, out_ref,
-    w_in, w_proj, acts, qkv, query, kv, high, total, accum, mixed, rope,
+    tok_ref, w_query_ref, w_keyval_ref, w_out_ref, len_ref, freq_ref, out_ref,
+    w_in, w_kv, w_proj, acts, qkv, query, kv, high, total, accum, mixed, rope,
     near_send, near_recv, part, far_send, far_recv,
     local_sem, in_send, in_recv, proj_send, proj_recv, bal_send,
     act_send, act_recv, kv_send, kv_recv, near_ss, near_rs, far_ss, far_rs,
@@ -36,7 +38,7 @@
     mate = y * 2 + 1 - core
     reach = n // 4
     tokens_own, width = tok_ref.shape
-    rows_in, in_cols = w_in_ref.shape
+    rows_in = w_query_ref.shape[0]
     rows_out = w_out_ref.shape[0]
     chunk_cols = w_out_ref.shape[1] // chunks
     block = tokens_own * heads
@@ -68,6 +70,9 @@
     def in_slot(i):
         return w_in.at[pl.ds(pl.multiple_of(i * rows_in, rows_in), rows_in)]
 
+    def kv_slot(i):
+        return w_kv.at[pl.ds(pl.multiple_of(i * rows_in, rows_in), rows_in)]
+
     def proj_slot(c, i):
         return w_proj.at[c, i]
 
@@ -76,7 +81,8 @@
 
     def stream(c):
         if c < 0:
-            return in_slot, w_in_ref, lambda d, r: in_send.at[d, r], lambda i: in_recv.at[i]
+            slot, source = (in_slot, w_query_ref) if c == QUERY else (kv_slot, kv_slot(b))
+            return slot, source, lambda d, r: in_send.at[c + 2, d, r], lambda i: in_recv.at[c + 2, i]
         return (
             functools.partial(proj_slot, c), proj_own(c),
             lambda d, r: proj_send.at[c, d, r], lambda i: proj_recv.at[c, i],
@@ -100,10 +106,12 @@
         ref = slot(origin)
         remote(ref, ref, ss(0, 0), rs(origin), target(ACROSS)).wait_recv()
 
+    twin = z + 1 - 2 * (z % 2)
+
     def crosses(c, row):
         if c < 0:
             return row >= 0
-        return jnp.logical_not(((z == 0) & (row == 1)) | ((z == steps - 1) & (row == steps - 2)))
+        return row != twin
 
     def line_own(c):
         @pl.when(z < steps - 1)
@@ -143,39 +151,38 @@
         def _():
             send_copy(c, ACROSS, z + s, False).start()
 
-    def side_copy(c, end):
+    def side_copy(c):
         ref = proj_slot(c, z * LINE + 1 - x)
-        return remote(ref, ref, bal_send.at[c, end], proj_recv.at[c, z * LINE + 1 - x],
-                      target(DOWN if end == 0 else UP))
+        return remote(ref, ref, bal_send.at[c], proj_recv.at[c, z * LINE + 1 - x],
+                      at_blk(twin * LINE + x))
 
     def balance(c):
-        @pl.when((z == 1) | (z == steps - 2))
+        @pl.when(twin < steps)
         def _():
             await_slot(c, z * LINE + 1 - x)
-
-        @pl.when(z == 1)
-        def _():
-            side_copy(c, 0).start()
-
-        @pl.when(z == steps - 2)
-        def _():
-            side_copy(c, 1).start()
+            side_copy(c).start()
 
     def await_crossed(c):
         def one(row, _):
-            already = ((z == 1) | (z == steps - 2)) & (row == z) & (c >= 0)
-
-            @pl.when(jnp.logical_not(already))
-            def _():
+            if c < 0:
                 await_slot(c, row * LINE + 1 - x)
+            else:
+                @pl.when((row != z) | (twin >= steps))
+                def _():
+                    await_slot(c, row * LINE + 1 - x)
             return 0
 
         lax.fori_loop(0, steps, one, 0)
 
-    line_own(-1)
-    cross_own(-1)
-    keep_in = pltpu.make_async_copy(w_in_ref, in_slot(b), local_sem.at[chunks])
+    line_own(QUERY)
+    cross_own(QUERY)
+    keep_in = pltpu.make_async_copy(w_query_ref, in_slot(b), local_sem.at[chunks])
     keep_in.start()
+    w_kv[pl.ds(pl.multiple_of(b * rows_in, rows_in), rows_in), :] = w_keyval_ref[...].reshape(
+        rows_in, w_kv.shape[1]
+    )
+    line_own(KEYVAL)
+    cross_own(KEYVAL)
     keep_out = [
         pltpu.make_async_copy(proj_own(c), proj_slot(c, b), local_sem.at[c]) for c in range(chunks)
     ]
@@ -208,8 +215,9 @@
     rope[1] = jnp.where(lane < HEAD_SIZE // 2, -jnp.sin(angle), jnp.sin(angle))
 
     def in_step(s, _):
-        line_step(-1, s)
-        cross_step(-1, s)
+        for c in (QUERY, KEYVAL):
+            line_step(c, s)
+            cross_step(c, s)
         return 0
 
     in_step(1, 0)
@@ -219,24 +227,25 @@
         copy = remote(acts.at[other], acts.at[other], act_send.at[outer + o], act_recv.at[other], at_head(mate))
         copy.start()
         act_copies.append(copy)
-    lax.fori_loop(2, steps, in_step, 0)
+    lax.fori_loop(2, steps - 1, in_step, 0)
 
     for c in range(chunks):
         line_own(c)
-    cross_own(0)
+    in_step(steps - 1, 0)
+    for c in range(chunks // 2):
+        cross_own(c)
     line_events = [(c, s) for s in range(1, steps) for c in range(chunks)]
 
     def run_events(count):
         for _ in range(min(count, len(line_events))):
             c, s = line_events.pop(0)
             line_step(c, s)
-            if c == 0:
-                cross_step(0, s)
-
-    run_events(2 * chunks - 1)
+
+    run_events(chunks + chunks // 2)
 
     keep_in.wait()
-    await_crossed(-1)
+    await_crossed(QUERY)
+    await_crossed(KEYVAL)
     for o in range(outer):
         other = lax.rem(y + o, outer) * 2 + 1 - core
         remote(acts.at[other], acts.at[other], act_send.at[0], act_recv.at[other], at_head(mate)).wait_recv()
@@ -246,8 +255,8 @@
     def project(k, _):
         cols = pl.ds(pl.multiple_of(k * depth, depth), depth)
         left = acts[:, :, cols].reshape(block, depth)
-        term = jnp.dot(left, w_in[cols, :], preferred_element_type=f32)
-        qkv[...] = term + qkv[...]
+        qkv[:, :q_cols] += jnp.dot(left, w_in[cols, :], preferred_element_type=f32)
+        qkv[:, q_cols:] += jnp.dot(left, w_kv[cols, :], preferred_element_type=f32)
         return 0
 
     qkv[...] = jnp.zeros_like(qkv)
@@ -274,7 +283,7 @@
         return 0
 
     lax.fori_loop(1, reach + 1, kv_start, 0)
-    run_events(chunks)
+    run_events(chunks - chunks // 2)
 
     scale = HEAD_SIZE ** (-0.5)
     high[...] = jnp.full_like(high, masked_score)
@@ -307,13 +316,18 @@
 
         lax.fori_loop(0, q_heads, one, 0)
 
-    attend(0)
-    run_events(len(line_events))
-    balance(0)
-    for c in range(1, chunks):
-        cross_own(c)
+    for c in range(chunks):
+        if c >= chunks // 2:
+            cross_own(c)
         for s in range(1, steps):
+            if (c, s) in line_events:
+                line_step(c, s)
             cross_step(c, s)
+        if c == 0:
+            attend(0)
+    early = min(2, chunks)
+    for c in range(early):
+        balance(c)
 
     def earlier(d, _):
         @pl.when(b >= d)
@@ -382,7 +396,7 @@
 
     for c in range(chunks):
         project_out(c)
-        if c + 1 < chunks:
+        if early <= c + 1 < chunks:
             balance(c + 1)
         if c > 0:
             finish(c - 1)
@@ -405,16 +419,12 @@
 
         lax.fori_loop(0, steps, one, 0)
 
-    for c in range(-1, chunks):
+    for c in range(KEYVAL, chunks):
         drain(c)
     for c in range(chunks):
-        @pl.when(z == 1)
-        def _():
-            side_copy(c, 0).wait_send()
-
-        @pl.when(z == steps - 2)
-        def _():
-            side_copy(c, 1).wait_send()
+        @pl.when(twin < steps)
+        def _():
+            side_copy(c).wait_send()
 
         near_copy(c).wait_send()
         for o in range(1, outer):
@@ -445,10 +455,9 @@
     chunk_cols = width // chunks
     q_heads = q_cols // HEAD_SIZE
     reach = n // 4
-    w_in = jnp.concatenate([w_query, key_value_weight.reshape(rows_in, kv_cols)], axis=1)
     half = HEAD_SIZE // 2
-    freqs = jnp.power(rope_base, -2.0 * jnp.arange(half, dtype=jnp.float32) / HEAD_SIZE)
-    freqs = jnp.concatenate([freqs, freqs])[None, :]
+    freqs = np.power(rope_base, -2.0 * np.arange(half) / HEAD_SIZE).astype(np.float32)
+    freqs = jnp.asarray(np.concatenate([freqs, freqs])[None, :])
     bf16, f32 = jnp.bfloat16, jnp.float32
     dma = pltpu.SemaphoreType.DMA
     return pl.pallas_call(
@@ -457,13 +466,15 @@
         in_specs=[
             pl.BlockSpec(memory_space=pltpu.VMEM),
             pl.BlockSpec(memory_space=pl.ANY),
+            pl.BlockSpec(memory_space=pltpu.VMEM),
             pl.BlockSpec(memory_space=pl.ANY),
             pl.BlockSpec(memory_space=pltpu.SMEM),
             pl.BlockSpec(memory_space=pltpu.VMEM),
         ],
         out_specs=pl.BlockSpec(memory_space=pltpu.VMEM),
         scratch_shapes=[
-            pltpu.VMEM((n * rows_in, q_cols + kv_cols), bf16),
+            pltpu.VMEM((n * rows_in, q_cols), bf16),
+            pltpu.VMEM((n * rows_in, kv_cols), bf16),
             pltpu.VMEM((chunks, n, rows_out, chunk_cols), bf16),
             pltpu.VMEM((heads, own, width), bf16),
             pltpu.VMEM((block, q_cols + kv_cols), f32),
@@ -480,11 +491,11 @@
             pltpu.VMEM((chunks, outer, own, chunk_cols), bf16),
             pltpu.VMEM((chunks, outer, own, chunk_cols), bf16),
             dma((chunks + 1,)),
-            dma((3, steps)),
-            dma((n,)),
+            dma((2, 3, steps)),
+            dma((2, n)),
             dma((chunks, 3, steps)),
             dma((chunks, n)),
-            dma((chunks, 2)),
+            dma((chunks,)),
             dma((2 * outer,)),
             dma((heads,)),
             dma((reach + 1,)),
@@ -497,7 +508,7 @@
         compiler_params=pltpu.CompilerParams(
             collective_id=0, has_side_effects=True, vmem_limit_bytes=60 * 1024 * 1024
         ),
-    )(tokens, w_in, w_out, doc_lengths, freqs)
+    )(tokens, w_query, key_value_weight, w_out, doc_lengths, freqs)
 
 
 def solution(mesh):

time: 152 us -> 144 us (0.947)
  Pallas kernels: 145 us -> 141 us
  other arithmetic: 2.65 us -> 0 us
    pallas_call x1, Pallas kernels: 145 us -> 141 us  [on_device(): pl.pallas_call(functools.partial(layer_kernel, n, heads, chunks), out_sha...]
    concatenate x1 -> x0, other arithmetic: 1.97 us -> none  [on_device(): jnp.concatenate([w_query, key_value_weight.reshape(rows_in, kv_cols)], ax...]
    unnamed x2 -> x1, local copies, waits for them, and re-layouts: 3.27 us -> 2.29 us
where the time goes in v2:
time: 144 us
  Pallas kernels  141 us (98%)
  local copies, waits for them, and re-layouts  2.29 us (2%)
    pallas_call x1, Pallas kernels, on_device(): pl.pallas_call(functools.partial(layer_kernel, n, heads, chunks), out_sha...  141 us

profile of v2, /device:TPU:27, one launch (start us, length us, event | category | flops | bytes accessed | tf_op | source)
XLA Modules:
  0.0 143.7 jit_solution(10434222267317909547)
XLA Ops:
  0.0 141.4 %shard_map.64 = bf16[128,4096]{1,0:T(8,128)(2,1)} custom-call(bf16[128,4096]{1,0:T(8,128)(2,1)} %tok_ref.1, bf16[512,512]{1,0:T(8,128)(2,1)} %w_query_ref.1, bf16[512,2,128]{2,1,0:T(2,128)(2,1)} %w_keyval_ref.1, bf16[64,4096]{1,0:T(8,128)(2,1)} %w_out_ref.1, s32[16]{0:T(128)} %len_ref.1, f32[1,128]{1,0:T(1,128)} %constant.2.clone.freq_ref), custom_call_target="tpu_custom_call" | custom-call | tf_op jit(solution)/shard_map/pallas_call | solution.py:463
  141.4 2.3 %copy.8 = bf16[128,4096]{1,0:T(8,128)(2,1)} copy(bf16[128,4096]{1,0:T(8,128)(2,1)} %shard_map.64) | data formatting | bytes 2097152

commit v3 on v2

--- a/solution.py
+++ b/solution.py
@@ -241,26 +241,57 @@
             c, s = line_events.pop(0)
             line_step(c, s)
 
-    run_events(chunks + chunks // 2)
-
     keep_in.wait()
-    await_crossed(QUERY)
-    await_crossed(KEYVAL)
     for o in range(outer):
         other = lax.rem(y + o, outer) * 2 + 1 - core
         remote(acts.at[other], acts.at[other], act_send.at[0], act_recv.at[other], at_head(mate)).wait_recv()
 
-    depth = min(512, width)
-
-    def project(k, _):
-        cols = pl.ds(pl.multiple_of(k * depth, depth), depth)
-        left = acts[:, :, cols].reshape(block, depth)
+    def project(k, size):
+        cols = pl.ds(pl.multiple_of(k * size, size), size)
+        left = acts[:, :, cols].reshape(block, size)
         qkv[:, :q_cols] += jnp.dot(left, w_in[cols, :], preferred_element_type=f32)
         qkv[:, q_cols:] += jnp.dot(left, w_kv[cols, :], preferred_element_type=f32)
-        return 0
 
     qkv[...] = jnp.zeros_like(qkv)
-    lax.fori_loop(0, width // depth, project, 0)
+
+    if rows_in % HEAD_SIZE == 0:
+        def lined(row, _):
+            project(row * LINE + x, rows_in)
+            return 0
+
+        def crossed_row(row):
+            origin = row * LINE + 1 - x
+            await_slot(QUERY, origin)
+            await_slot(KEYVAL, origin)
+            project(origin, rows_in)
+
+        def crossed(s, _):
+            @pl.when(z - s >= 0)
+            def _():
+                crossed_row(z - s)
+
+            @pl.when(z + s <= steps - 1)
+            def _():
+                crossed_row(z + s)
+            return 0
+
+        lax.fori_loop(0, steps, lined, 0)
+        crossed_row(z)
+        run_events(chunks)
+        lax.fori_loop(1, steps - 1, crossed, 0)
+        run_events(chunks // 2)
+        crossed(steps - 1, 0)
+    else:
+        run_events(chunks + chunks // 2)
+        await_crossed(QUERY)
+        await_crossed(KEYVAL)
+        depth = min(512, width)
+
+        def whole_step(k, _):
+            project(k, depth)
+            return 0
+
+        lax.fori_loop(0, width // depth, whole_step, 0)
 
     cosine, sine = rope[0], rope[1]
 

time: 144 us -> 144 us (level)
  no operation moved by 1% of the time
where the time goes in v3:
time: 144 us
  Pallas kernels  141 us (98%)
  local copies, waits for them, and re-layouts  2.29 us (2%)
    pallas_call x1, Pallas kernels, on_device(): pl.pallas_call(functools.partial(layer_kernel, n, heads, chunks), out_sha...  141 us

profile of v3, /device:TPU:27, one launch (start us, length us, event | category | flops | bytes accessed | tf_op | source)
XLA Modules:
  0.0 143.7 jit_solution(410586727560430202)
XLA Ops:
  0.0 141.4 %shard_map.64 = bf16[128,4096]{1,0:T(8,128)(2,1)} custom-call(bf16[128,4096]{1,0:T(8,128)(2,1)} %tok_ref.1, bf16[512,512]{1,0:T(8,128)(2,1)} %w_query_ref.1, bf16[512,2,128]{2,1,0:T(2,128)(2,1)} %w_keyval_ref.1, bf16[64,4096]{1,0:T(8,128)(2,1)} %w_out_ref.1, s32[16]{0:T(128)} %len_ref.1, f32[1,128]{1,0:T(1,128)} %constant.2.clone.freq_ref), custom_call_target="tpu_custom_call" | custom-call | tf_op jit(solution)/shard_map/pallas_call | solution.py:494
  141.4 2.3 %copy.8 = bf16[128,4096]{1,0:T(8,128)(2,1)} copy(bf16[128,4096]{1,0:T(8,128)(2,1)} %shard_map.64) | data formatting | bytes 2097152
